TPU v7x, 32 devices: a whole 2x2x4 slice. The times are simulated.
32 devices in a mesh: tensor: 4 (over y, x), dp: 8 (over z, core).
Axes of the slice: x: 2, y: 2, z: 4, core: 2. Of those that a mesh axis runs over, the one named last changes fastest.
Arguments:
- images: bfloat16 [32, 729, 1152], P('dp'), may hold values from -16 to 16
- counts: int32 [8], P('dp'), may hold values from 3 to 4, as said below
- ln1_gain: bfloat16 [1152], replicated, may hold values from 0.099609375 to 1.8984375
- ln1_bias: bfloat16 [1152], replicated, may hold values from -3 to 3
- qkv_weight: bfloat16 [3, 1152, 1152], P(None, None, 'tensor'), may hold values from -1 to 1
- qv_bias: bfloat16 [2, 1152], P(None, 'tensor'), may hold values from -3 to 3
- out_weight: bfloat16 [1152, 1152], P('tensor'), may hold values from -1.5 to 1.5
- out_bias: bfloat16 [1152], replicated, may hold values from -3 to 3
- ln2_gain: bfloat16 [1152], replicated, may hold values from 0.099609375 to 1.8984375
- ln2_bias: bfloat16 [1152], replicated, may hold values from -3 to 3
- fc1_weight: bfloat16 [1152, 4304], P(None, 'tensor'), may hold values from -0.1875 to 0.1875
- fc1_bias: bfloat16 [4304], P('tensor'), may hold values from -3 to 3
- fc2_weight: bfloat16 [4304, 1152], P('tensor'), may hold values from -0.25 to 0.25
- fc2_bias: bfloat16 [1152], replicated, may hold values from -3 to 3
- grad_out: bfloat16 [32, 729, 1152], P('dp'), may hold values from -6 to 6
Outputs:
- block_out: float32 [32, 729, 1152], P('dp', None, 'tensor')
- grad_in: float32 [32, 729, 1152], P('dp', None, 'tensor')
- grad_ln1_gain: float32 [1152], P('tensor')
- grad_ln1_bias: float32 [1152], P('tensor')
- grad_qkv_weight: float32 [3, 1152, 1152], P(None, None, 'tensor')
- grad_qv_bias: float32 [2, 1152], P(None, 'tensor')
- grad_out_weight: float32 [1152, 1152], P('tensor')
- grad_out_bias: float32 [1152], P('tensor')
- grad_ln2_gain: float32 [1152], P('tensor')
- grad_ln2_bias: float32 [1152], P('tensor')
- grad_fc1_weight: float32 [1152, 4304], P(None, 'tensor')
- grad_fc1_bias: float32 [4304], P('tensor')
- grad_fc2_weight: float32 [4304, 1152], P('tensor')
- grad_fc2_bias: float32 [1152], P('tensor')
Inputs may be any that keep to these rules, and one draw needn't show every extreme that they name: `counts`: exactly 6 of the 8 replicas hold 4 live images, the others 4 - 1; a replica's live images fill its first slots.
All inputs are finite; a program needn't handle non-finite values.
Results may differ from a plain program's by a relative error of at most 0.02.
Values may be sent and summed in bfloat16 or wider, within the bound.
A program may use at most 192 MiB of HBM per device.

v0:
```python
import math
import jax
import jax.numpy as jnp
from jax import lax
from jax.sharding import PartitionSpec as P

HD = 72
EPS = 1e-06


def own_columns(values, share_width):
    start = lax.axis_index("tensor") * share_width
    return lax.dynamic_slice_in_dim(values, start, share_width, values.ndim - 1)


def row_mean(values):
    return jnp.mean(values, axis=-1, keepdims=True)


def group_stats(first, second):
    return lax.psum((first, second), "tensor")


def contract_rows(left, right):
    return lax.dot_general(
        left, right, (((0,), (0,)), ((), ())), preferred_element_type=jnp.float32
    )


def contract_cols(left, right):
    return lax.dot_general(
        left, right, (((1,), (1,)), ((), ())), preferred_element_type=jnp.float32
    )


def gelu_tanh(values):
    return jax.nn.gelu(values, approximate=True)


def local(
    images,
    counts,
    ln1_gain,
    ln1_bias,
    qkv_weight,
    qv_bias,
    out_weight,
    out_bias,
    ln2_gain,
    ln2_bias,
    fc1_weight,
    fc1_bias,
    fc2_weight,
    fc2_bias,
    grad_out,
):
    slot_count, length, full_width = images.shape
    share_width = full_width // lax.axis_size("tensor")
    local_width = qkv_weight.shape[2]
    local_heads = local_width // HD
    hidden_width = fc1_weight.shape[1]
    score_scale = 1.0 / math.sqrt(HD)
    gain_one = ln1_gain.astype(jnp.float32)
    shift_one = ln1_bias.astype(jnp.float32)
    gain_two = ln2_gain.astype(jnp.float32)
    shift_two = ln2_bias.astype(jnp.float32)
    bias_out = out_bias.astype(jnp.float32)
    bias_fc1 = fc1_bias.astype(jnp.float32)
    bias_fc2 = fc2_bias.astype(jnp.float32)
    bias_query = qv_bias[0].astype(jnp.float32)
    bias_value = qv_bias[1].astype(jnp.float32)
    live_count = counts[0]

    def to_heads(values):
        return values.reshape(length, local_heads, HD)

    def head_scores(query_heads, key_heads):
        return (
            jnp.einsum("qhd,khd->hqk", query_heads, key_heads, preferred_element_type=jnp.float32)
            * score_scale
        )

    def layer_step(slot_index, loop_state):
        block_acc, input_acc, grads = loop_state
        (
            grad_gain_one,
            grad_shift_one,
            grad_qkv,
            grad_qv,
            grad_out_w,
            grad_out_b,
            grad_gain_two,
            grad_shift_two,
            grad_fc1_w,
            grad_fc1_b,
            grad_fc2_w,
            grad_fc2_b,
        ) = grads
        live_flag = (slot_index < live_count).astype(jnp.float32)
        picture = lax.dynamic_index_in_dim(images, slot_index, 0, keepdims=False).astype(
            jnp.float32
        )
        upstream = (
            lax.dynamic_index_in_dim(grad_out, slot_index, 0, keepdims=False).astype(jnp.float32)
            * live_flag
        )
        upstream_low = upstream.astype(jnp.bfloat16)
        centered = picture - row_mean(picture)
        inv_one = lax.rsqrt(row_mean(centered * centered) + EPS)
        unit_one = centered * inv_one
        normed_one = (unit_one * gain_one + shift_one).astype(jnp.bfloat16)
        query_rows = (
            jnp.dot(normed_one, qkv_weight[0], preferred_element_type=jnp.float32) + bias_query
        ).astype(jnp.bfloat16)
        key_rows = jnp.dot(normed_one, qkv_weight[1], preferred_element_type=jnp.float32).astype(
            jnp.bfloat16
        )
        value_rows = (
            jnp.dot(normed_one, qkv_weight[2], preferred_element_type=jnp.float32) + bias_value
        ).astype(jnp.bfloat16)
        query_heads = to_heads(query_rows)
        key_heads = to_heads(key_rows)
        value_heads = to_heads(value_rows)
        scores = head_scores(query_heads, key_heads)
        row_top = jnp.max(scores, axis=-1, keepdims=True)
        logsum = row_top + jnp.log(jnp.sum(jnp.exp(scores - row_top), axis=-1, keepdims=True))
        probs_low = jnp.exp(scores - logsum).astype(jnp.bfloat16)
        mixed = jnp.einsum(
            "hqk,khd->qhd", probs_low, value_heads, preferred_element_type=jnp.float32
        )
        mixed = mixed.reshape(length, local_width).astype(jnp.bfloat16)
        partial_out = jnp.dot(mixed, out_weight, preferred_element_type=jnp.float32).astype(
            jnp.bfloat16
        )
        residual = (
            own_columns(picture, share_width)
            + lax.psum_scatter(partial_out, "tensor", scatter_dimension=1, tiled=True).astype(
                jnp.float32
            )
            + own_columns(bias_out, share_width)
        )
        row_sum, row_square = group_stats(
            jnp.sum(residual, axis=-1), jnp.sum(residual * residual, axis=-1)
        )
        average = row_sum[:, None] / full_width
        inv_two = lax.rsqrt(row_square[:, None] / full_width - average * average + EPS)
        unit_two = (residual - average) * inv_two
        own_normed = (
            unit_two * own_columns(gain_two, share_width) + own_columns(shift_two, share_width)
        ).astype(jnp.bfloat16)
        normed_two = lax.all_gather(own_normed, "tensor", axis=1, tiled=True)
        preact = jnp.dot(normed_two, fc1_weight, preferred_element_type=jnp.float32) + bias_fc1
        activated = gelu_tanh(preact).astype(jnp.bfloat16)
        partial_mlp = jnp.dot(activated, fc2_weight, preferred_element_type=jnp.float32).astype(
            jnp.bfloat16
        )
        block_rows = (
            residual
            + lax.psum_scatter(partial_mlp, "tensor", scatter_dimension=1, tiled=True).astype(
                jnp.float32
            )
            + own_columns(bias_fc2, share_width)
        )
        block_rows = block_rows * live_flag
        grad_fc2_b = grad_fc2_b + own_columns(jnp.sum(upstream, axis=0), share_width)
        grad_fc2_w = grad_fc2_w + contract_rows(activated, upstream_low)
        d_act = contract_cols(upstream_low, fc2_weight)
        gelu_pull = jax.vjp(gelu_tanh, preact)[1]
        d_pre = gelu_pull(d_act)[0].astype(jnp.bfloat16)
        grad_fc1_b = grad_fc1_b + jnp.sum(d_pre.astype(jnp.float32), axis=0)
        grad_fc1_w = grad_fc1_w + contract_rows(normed_two, d_pre)
        back_mlp = contract_cols(d_pre, fc1_weight)
        d_norm_two = lax.psum_scatter(
            back_mlp.astype(jnp.bfloat16), "tensor", scatter_dimension=1, tiled=True
        ).astype(jnp.float32)
        scaled_two = d_norm_two * own_columns(gain_two, share_width)
        sum_plain, sum_cross = group_stats(
            jnp.sum(scaled_two, axis=-1), jnp.sum(scaled_two * unit_two, axis=-1)
        )
        d_residual = own_columns(upstream, share_width) + inv_two * (
            scaled_two
            - sum_plain[:, None] / full_width
            - unit_two * (sum_cross[:, None] / full_width)
        )
        grad_gain_two = grad_gain_two + jnp.sum(d_norm_two * unit_two, axis=0)
        grad_shift_two = grad_shift_two + jnp.sum(d_norm_two, axis=0)
        grad_out_b = grad_out_b + jnp.sum(d_residual, axis=0)
        d_residual_low = lax.all_gather(
            d_residual.astype(jnp.bfloat16), "tensor", axis=1, tiled=True
        )
        grad_out_w = grad_out_w + contract_rows(mixed, d_residual_low)
        d_mixed_heads = to_heads(contract_cols(d_residual_low, out_weight).astype(jnp.bfloat16))
        probs = jnp.exp(head_scores(query_heads, key_heads) - logsum)
        probs_again = probs.astype(jnp.bfloat16)
        d_value = jnp.einsum(
            "hqk,qhd->khd", probs_again, d_mixed_heads, preferred_element_type=jnp.float32
        )
        d_probs = jnp.einsum(
            "qhd,khd->hqk", d_mixed_heads, value_heads, preferred_element_type=jnp.float32
        )
        inner = jnp.sum(probs * d_probs, axis=-1, keepdims=True)
        d_scores = (probs * (d_probs - inner)).astype(jnp.bfloat16)
        d_query = (
            jnp.einsum("hqk,khd->qhd", d_scores, key_heads, preferred_element_type=jnp.float32)
            * score_scale
        )
        d_key = (
            jnp.einsum("hqk,qhd->khd", d_scores, query_heads, preferred_element_type=jnp.float32)
            * score_scale
        )
        d_stack = (
            jnp.stack([d_query, d_key, d_value], axis=1)
            .reshape(length, 3, local_width)
            .astype(jnp.bfloat16)
        )
        grad_qkv = grad_qkv + jnp.einsum(
            "ld,lje->jde", normed_one, d_stack, preferred_element_type=jnp.float32
        )
        bias_sums = jnp.sum(d_stack.astype(jnp.float32), axis=0)
        grad_qv = grad_qv + jnp.stack([bias_sums[0], bias_sums[2]])
        back_attn = jnp.einsum(
            "lje,jde->ld", d_stack, qkv_weight, preferred_element_type=jnp.float32
        )
        d_norm_one = lax.psum_scatter(
            back_attn.astype(jnp.bfloat16), "tensor", scatter_dimension=1, tiled=True
        ).astype(jnp.float32)
        own_unit = own_columns(unit_one, share_width)
        scaled_one = d_norm_one * own_columns(gain_one, share_width)
        plain_one, cross_one = group_stats(
            jnp.sum(scaled_one, axis=-1), jnp.sum(scaled_one * own_unit, axis=-1)
        )
        d_input = d_residual + inv_one * (
            scaled_one
            - plain_one[:, None] / full_width
            - own_unit * (cross_one[:, None] / full_width)
        )
        grad_gain_one = grad_gain_one + jnp.sum(d_norm_one * own_unit, axis=0)
        grad_shift_one = grad_shift_one + jnp.sum(d_norm_one, axis=0)
        block_acc = lax.dynamic_update_index_in_dim(block_acc, block_rows, slot_index, 0)
        input_acc = lax.dynamic_update_index_in_dim(input_acc, d_input, slot_index, 0)
        new_grads = (
            grad_gain_one,
            grad_shift_one,
            grad_qkv,
            grad_qv,
            grad_out_w,
            grad_out_b,
            grad_gain_two,
            grad_shift_two,
            grad_fc1_w,
            grad_fc1_b,
            grad_fc2_w,
            grad_fc2_b,
        )
        return (block_acc, input_acc, new_grads)

    share_zeros = jnp.zeros((share_width,), jnp.float32)
    start_grads = (
        share_zeros,
        share_zeros,
        jnp.zeros((3, full_width, local_width), jnp.float32),
        jnp.zeros((2, local_width), jnp.float32),
        jnp.zeros((local_width, full_width), jnp.float32),
        share_zeros,
        share_zeros,
        share_zeros,
        jnp.zeros((full_width, hidden_width), jnp.float32),
        jnp.zeros((hidden_width,), jnp.float32),
        jnp.zeros((hidden_width, full_width), jnp.float32),
        share_zeros,
    )
    start_rows = jnp.zeros((slot_count, length, share_width), jnp.float32)
    block_acc, input_acc, grads = lax.fori_loop(
        0, slot_count, layer_step, (start_rows, start_rows, start_grads)
    )
    (
        grad_gain_one,
        grad_shift_one,
        grad_qkv,
        grad_qv,
        grad_out_w,
        grad_out_b,
        grad_gain_two,
        grad_shift_two,
        grad_fc1_w,
        grad_fc1_b,
        grad_fc2_w,
        grad_fc2_b,
    ) = grads
    summed = (
        lax.psum(grad_gain_one.astype(jnp.bfloat16), "dp").astype(jnp.float32),
        lax.psum(grad_shift_one.astype(jnp.bfloat16), "dp").astype(jnp.float32),
        lax.psum(grad_qkv.astype(jnp.bfloat16), "dp").astype(jnp.float32),
        lax.psum(grad_qv.astype(jnp.bfloat16), "dp").astype(jnp.float32),
        lax.psum(grad_out_w.astype(jnp.bfloat16), "dp").astype(jnp.float32),
        lax.psum(grad_out_b.astype(jnp.bfloat16), "dp").astype(jnp.float32),
        lax.psum(grad_gain_two.astype(jnp.bfloat16), "dp").astype(jnp.float32),
        lax.psum(grad_shift_two.astype(jnp.bfloat16), "dp").astype(jnp.float32),
        lax.psum(grad_fc1_w.astype(jnp.bfloat16), "dp").astype(jnp.float32),
        lax.psum(grad_fc1_b.astype(jnp.bfloat16), "dp").astype(jnp.float32),
        lax.psum(grad_fc2_w.astype(jnp.bfloat16), "dp").astype(jnp.float32),
        lax.psum(grad_fc2_b.astype(jnp.bfloat16), "dp").astype(jnp.float32),
    )
    return (
        block_acc,
        input_acc,
        summed[0],
        summed[1],
        summed[2],
        summed[3],
        summed[4],
        summed[5],
        summed[6],
        summed[7],
        summed[8],
        summed[9],
        summed[10],
        summed[11],
    )


def solution(mesh):
    return jax.shard_map(
        local,
        mesh=mesh,
        in_specs=(
            P("dp", None, None),
            P("dp"),
            P(),
            P(),
            P(None, None, "tensor"),
            P(None, "tensor"),
            P("tensor", None),
            P(),
            P(),
            P(),
            P(None, "tensor"),
            P("tensor"),
            P("tensor", None),
            P(),
            P("dp", None, None),
        ),
        out_specs=(
            P("dp", None, "tensor"),
            P("dp", None, "tensor"),
            P("tensor"),
            P("tensor"),
            P(None, None, "tensor"),
            P(None, "tensor"),
            P("tensor", None),
            P("tensor"),
            P("tensor"),
            P("tensor"),
            P(None, "tensor"),
            P("tensor"),
            P("tensor", None),
            P("tensor"),
        ),
        check_vma=False,
    )
```

profile of v0, /device:TPU:0, one launch (start us, length us, event | category | flops | bytes accessed | tf_op | source)
XLA Modules:
  0.0 1362.5 jit_solution(6711157673283328373)
XLA Ops:
  16.7 12.7 copy.34
  29.4 12.7 copy.35
  42.1 1129.5 %while.42 = (s32[]{:T(128)}, f32[4,729,288]{1,2,0:T(8,128)}, f32[4,729,288]{1,2,0:T(8,128)}, f32[288]{0:T(512)}, f32[288]{0:T(512)}, /*index=5*/f32[3,1152,288]{...) while((s32[]{:T(128)}, f32[4,729,288]{1,2,0:T(8,128)}, ...), condition=%wide.region_30.31_spmd.clone, body=%wide.region_0.30_spmd.clone.sunk | while | flops 18614964224 | bytes 394633504 | solution.py:273
  70.5 29.5 %reduce-scatter.5.cloned.1.call-done = bf16[729,288]{0,1:T(8,128)(2,1)} async-done(((bf16[729,1152]{0,1:T(8,128)(2,1)}), bf16[729,288]{0,1:T(8,128)(2,1)}) %reduce-scatter.5.cloned.1.call-update) | async-done | bytes 419920 | tf_op jit(solution)/shard_map/while/body/eval_jaxpr/reduce_scatter | solution.py:137
  101.5 9.1 all-reduce.8
  112.9 31.3 %all-gather.3.cloned.1.call-done = bf16[729,1152]{0,1:T(8,128)(2,1)} async-done(((bf16[729,288]{0,1:T(8,128)(2,1)}), bf16[729,1152]{0,1:T(8,128)(2,1)}) %all-gather.3.cloned.1.call-update) | async-done | bytes 1679632 | tf_op jit(solution)/shard_map/while/body/eval_jaxpr/all_gather | solution.py:151
  149.0 7.7 convert_reduce_fusion.11
  165.4 29.0 %reduce-scatter.9.cloned.1.call-done = bf16[729,288]{0,1:T(8,128)(2,1)} async-done(((bf16[729,1152]{0,1:T(8,128)(2,1)}), bf16[729,288]{0,1:T(8,128)(2,1)}) %reduce-scatter.9.cloned.1.call-update) | async-done | bytes 419920 | tf_op jit(solution)/shard_map/while/body/eval_jaxpr/reduce_scatter | solution.py:173
  196.4 9.1 all-reduce.9
  215.2 6.1 convolution_convert_fusion.17
  221.4 19.9 %all-gather.5.cloned.1.call-done = bf16[729,1152]{0,1:T(8,128)(2,1)} async-done(((bf16[729,288]{0,1:T(8,128)(2,1)}), bf16[729,1152]{0,1:T(8,128)(2,1)}) %all-gather.5.cloned.1.call-update) | async-done | bytes 1679632 | tf_op jit(solution)/shard_map/while/body/eval_jaxpr/all_gather | solution.py:188
  243.7 7.6 multiply_reduce_fusion.9
  251.3 10.4 multiply_convert_fusion.9
  266.8 5.7 convolution_convert_fusion.20
  278.1 6.8 convolution_add_fusion.12
  285.5 6.9 convolution_add_fusion.13
  299.2 6.0 bitcast_add_fusion.3
  305.2 6.9 reduce-scatter.11.cloned.1.call-done
  313.8 9.1 all-reduce.10
  354.3 26.8 %reduce-scatter.5.cloned.1.call-done = bf16[729,288]{0,1:T(8,128)(2,1)} async-done(((bf16[729,1152]{0,1:T(8,128)(2,1)}), bf16[729,288]{0,1:T(8,128)(2,1)}) %reduce-scatter.5.cloned.1.call-update) | async-done | bytes 419920 | tf_op jit(solution)/shard_map/while/body/eval_jaxpr/reduce_scatter | solution.py:137
  382.6 9.1 all-reduce.8
  393.6 31.7 %all-gather.3.cloned.1.call-done = bf16[729,1152]{0,1:T(8,128)(2,1)} async-done(((bf16[729,288]{0,1:T(8,128)(2,1)}), bf16[729,1152]{0,1:T(8,128)(2,1)}) %all-gather.3.cloned.1.call-update) | async-done | bytes 1679632 | tf_op jit(solution)/shard_map/while/body/eval_jaxpr/all_gather | solution.py:151
  430.1 7.7 convert_reduce_fusion.11
  446.5 29.0 %reduce-scatter.9.cloned.1.call-done = bf16[729,288]{0,1:T(8,128)(2,1)} async-done(((bf16[729,1152]{0,1:T(8,128)(2,1)}), bf16[729,288]{0,1:T(8,128)(2,1)}) %reduce-scatter.9.cloned.1.call-update) | async-done | bytes 419920 | tf_op jit(solution)/shard_map/while/body/eval_jaxpr/reduce_scatter | solution.py:173
  477.4 9.1 all-reduce.9
  496.9 6.1 convolution_convert_fusion.17
  503.1 19.2 %all-gather.5.cloned.1.call-done = bf16[729,1152]{0,1:T(8,128)(2,1)} async-done(((bf16[729,288]{0,1:T(8,128)(2,1)}), bf16[729,1152]{0,1:T(8,128)(2,1)}) %all-gather.5.cloned.1.call-update) | async-done | bytes 1679632 | tf_op jit(solution)/shard_map/while/body/eval_jaxpr/all_gather | solution.py:188
  524.8 7.6 multiply_reduce_fusion.9
  532.4 10.3 multiply_convert_fusion.9
  559.2 8.2 convolution_add_fusion.12
  568.1 8.4 convolution_add_fusion.13
  584.7 7.2 bitcast_add_fusion.3
  595.1 9.1 all-reduce.10
  635.3 26.8 %reduce-scatter.5.cloned.1.call-done = bf16[729,288]{0,1:T(8,128)(2,1)} async-done(((bf16[729,1152]{0,1:T(8,128)(2,1)}), bf16[729,288]{0,1:T(8,128)(2,1)}) %reduce-scatter.5.cloned.1.call-update) | async-done | bytes 419920 | tf_op jit(solution)/shard_map/while/body/eval_jaxpr/reduce_scatter | solution.py:137
  663.6 9.1 all-reduce.8
  674.9 31.5 %all-gather.3.cloned.1.call-done = bf16[729,1152]{0,1:T(8,128)(2,1)} async-done(((bf16[729,288]{0,1:T(8,128)(2,1)}), bf16[729,1152]{0,1:T(8,128)(2,1)}) %all-gather.3.cloned.1.call-update) | async-done | bytes 1679632 | tf_op jit(solution)/shard_map/while/body/eval_jaxpr/all_gather | solution.py:151
  711.1 7.7 convert_reduce_fusion.11
  727.5 29.0 %reduce-scatter.9.cloned.1.call-done = bf16[729,288]{0,1:T(8,128)(2,1)} async-done(((bf16[729,1152]{0,1:T(8,128)(2,1)}), bf16[729,288]{0,1:T(8,128)(2,1)}) %reduce-scatter.9.cloned.1.call-update) | async-done | bytes 419920 | tf_op jit(solution)/shard_map/while/body/eval_jaxpr/reduce_scatter | solution.py:173
  758.5 9.1 all-reduce.9
  778.0 6.1 convolution_convert_fusion.17
  784.2 19.2 %all-gather.5.cloned.1.call-done = bf16[729,1152]{0,1:T(8,128)(2,1)} async-done(((bf16[729,288]{0,1:T(8,128)(2,1)}), bf16[729,1152]{0,1:T(8,128)(2,1)}) %all-gather.5.cloned.1.call-update) | async-done | bytes 1679632 | tf_op jit(solution)/shard_map/while/body/eval_jaxpr/all_gather | solution.py:188
  805.8 7.6 multiply_reduce_fusion.9
  813.4 10.4 multiply_convert_fusion.9
  828.9 5.7 convolution_convert_fusion.20
  840.3 8.2 convolution_add_fusion.12
  849.1 8.2 convolution_add_fusion.13
  865.5 7.2 bitcast_add_fusion.3
  875.9 9.1 all-reduce.10
  916.5 26.8 %reduce-scatter.5.cloned.1.call-done = bf16[729,288]{0,1:T(8,128)(2,1)} async-done(((bf16[729,1152]{0,1:T(8,128)(2,1)}), bf16[729,288]{0,1:T(8,128)(2,1)}) %reduce-scatter.5.cloned.1.call-update) | async-done | bytes 419920 | tf_op jit(solution)/shard_map/while/body/eval_jaxpr/reduce_scatter | solution.py:137
  944.8 9.1 all-reduce.8
  955.7 31.7 %all-gather.3.cloned.1.call-done = bf16[729,1152]{0,1:T(8,128)(2,1)} async-done(((bf16[729,288]{0,1:T(8,128)(2,1)}), bf16[729,1152]{0,1:T(8,128)(2,1)}) %all-gather.3.cloned.1.call-update) | async-done | bytes 1679632 | tf_op jit(solution)/shard_map/while/body/eval_jaxpr/all_gather | solution.py:151
  992.2 7.7 convert_reduce_fusion.11
  1008.6 29.0 %reduce-scatter.9.cloned.1.call-done = bf16[729,288]{0,1:T(8,128)(2,1)} async-done(((bf16[729,1152]{0,1:T(8,128)(2,1)}), bf16[729,288]{0,1:T(8,128)(2,1)}) %reduce-scatter.9.cloned.1.call-update) | async-done | bytes 419920 | tf_op jit(solution)/shard_map/while/body/eval_jaxpr/reduce_scatter | solution.py:173
  1039.6 9.1 all-reduce.9
  1059.1 6.1 convolution_convert_fusion.17
  1065.3 19.2 %all-gather.5.cloned.1.call-done = bf16[729,1152]{0,1:T(8,128)(2,1)} async-done(((bf16[729,288]{0,1:T(8,128)(2,1)}), bf16[729,1152]{0,1:T(8,128)(2,1)}) %all-gather.5.cloned.1.call-update) | async-done | bytes 1679632 | tf_op jit(solution)/shard_map/while/body/eval_jaxpr/all_gather | solution.py:188
  1086.9 7.6 multiply_reduce_fusion.9
  1094.5 10.3 multiply_convert_fusion.9
  1121.4 8.2 convolution_add_fusion.12
  1130.3 8.4 convolution_add_fusion.13
  1146.8 7.2 bitcast_add_fusion.3
  1157.2 9.1 all-reduce.10
  1184.1 27.8 %all-reduce.3 = (bf16[288]{0:T(512)(128)(2,1)S(1)}, bf16[288]{0:T(512)(128)(2,1)S(1)}, bf16[2,288]{1,0:T(2,128)(2,1)S(1)}, bf16[288]{0:T(512)(128)(2,1)S(1)}, bf...) all-reduce(bf16[288]{0:T(512)(128)(2,1)S(1)} %convert_element_type., ...), channel_id=1, replica_groups=mesh['tensor'=4,'dp'=8] {'dp'}, use_global_device_ids=true, to_apply=%region_31.32 | all-reduce | flops 3380 | bytes 13520 | tf_op jit(solution)/shard_map/psum | solution.py:291
  1216.5 127.7 %all-reduce.13.cloned.1.call-done = (bf16[3,1152,288]{1,2,0:T(8,128)(2,1)}, bf16[288,1152]{1,0:T(8,128)(2,1)}, bf16[1152,1076]{0,1:T(8,128)(2,1)}, bf16[1076,1152]{1,0:T(8,128)(2,1)}) async-done(((bf16[3,1152,288]{1,2,0:T(8,128)(2,1)}, bf16[288,1152]{1,0:T(8,128)(2,1)}, bf16[1152,1076]{0,1:T(8,128)(2,1)}, bf16[1076,1152]{1,0:T(8,128)(2,1)}), (bf16[3,1152,288]{1,2,0:T(8,128)(2,1)}, ...) | async-done | bytes 7612432 | tf_op jit(solution)/shard_map/psum | solution.py:293
  (640 shorter events, 382.3 us)
Async XLA Ops:
  42.1 9.8 copy-start.41
  42.1 166.6 %copy-start.18 = (f32[1152]{0:T(1024)}, f32[1152]{0:T(1024)S(1)}, u32[]{:S(2)}) copy-start(f32[1152]{0:T(1024)S(1)} %get-tuple-element.1334) | copy-start | bytes 13828 | tf_op jit(solution)/shard_map/while
  42.1 57.8 %reduce-scatter.5.cloned.1.call-start = ((), (), s32[]{:S(2)}) async-start(), calls=%async_computation.5 | async-start | bytes 2211840 | tf_op jit(solution)/shard_map/while/body/eval_jaxpr/reduce_scatter | solution.py:137
  44.0 167.6 %copy-start.15 = (f32[729]{0:T(1024)}, f32[729]{0:T(1024)S(1)}, u32[]{:S(2)}) copy-start(f32[729]{0:T(1024)S(1)} %broadcast_multiply_fusion.11) | copy-start | bytes 8752 | tf_op jit(solution)/shard_map/while
  64.6 79.6 %all-gather.3.cloned.1.call-start = ((), (), s32[]{:S(2)}) async-start(), calls=%async_computation.6 | async-start | bytes 2211840 | tf_op jit(solution)/shard_map/while/body/eval_jaxpr/all_gather | solution.py:151
  111.6 82.7 %reduce-scatter.9.cloned.1.call-start = ((), (), s32[]{:S(2)}) async-start(), calls=%async_computation.8 | async-start | bytes 2211840 | tf_op jit(solution)/shard_map/while/body/eval_jaxpr/reduce_scatter | solution.py:173
  161.7 79.5 %all-gather.5.cloned.1.call-start = ((), (), s32[]{:S(2)}) async-start(), calls=%async_computation.9 | async-start | bytes 2211840 | tf_op jit(solution)/shard_map/while/body/eval_jaxpr/all_gather | solution.py:188
  208.7 84.9 %reduce-scatter.7.cloned.1.call-start = ((), (), s32[]{:S(2)}) async-start(), calls=%async_computation.7 | async-start | bytes 2211840 | tf_op jit(solution)/shard_map/while/body/eval_jaxpr/reduce_scatter | solution.py:159
  221.3 90.8 %reduce-scatter.11.cloned.1.call-start = ((), (), s32[]{:S(2)}) async-start(), calls=%async_computation.10 | async-start | bytes 2211840 | tf_op jit(solution)/shard_map/while/body/eval_jaxpr/reduce_scatter | solution.py:224
  299.2 12.9 copy-start.17
  299.2 23.7 %copy-start.30 = (f32[288]{0:T(512)S(1)}, f32[288]{0:T(512)}, u32[]{:S(2)}) copy-start(f32[288]{0:T(512)} %get-tuple-element.1286) | copy-start | bytes 3460 | tf_op jit(solution)/shard_map/while
  299.2 23.7 %copy-start.33 = (f32[288]{0:T(512)S(1)}, f32[288]{0:T(512)}, u32[]{:S(2)}) copy-start(f32[288]{0:T(512)} %get-tuple-element.1285) | copy-start | bytes 3460 | tf_op jit(solution)/shard_map/while
  312.1 13.4 copy-start.19
  312.1 13.4 copy-start.21
  312.1 13.4 copy-start.40
  312.1 13.4 copy-start.42
  325.9 9.8 copy-start.41
  325.9 163.9 %copy-start.18 = (f32[1152]{0:T(1024)}, f32[1152]{0:T(1024)S(1)}, u32[]{:S(2)}) copy-start(f32[1152]{0:T(1024)S(1)} %get-tuple-element.1334) | copy-start | bytes 13828 | tf_op jit(solution)/shard_map/while
  325.9 55.1 %reduce-scatter.5.cloned.1.call-start = ((), (), s32[]{:S(2)}) async-start(), calls=%async_computation.5 | async-start | bytes 2211840 | tf_op jit(solution)/shard_map/while/body/eval_jaxpr/reduce_scatter | solution.py:137
  327.8 165.5 %copy-start.15 = (f32[729]{0:T(1024)}, f32[729]{0:T(1024)S(1)}, u32[]{:S(2)}) copy-start(f32[729]{0:T(1024)S(1)} %broadcast_multiply_fusion.11) | copy-start | bytes 8752 | tf_op jit(solution)/shard_map/while
  348.4 76.9 %all-gather.3.cloned.1.call-start = ((), (), s32[]{:S(2)}) async-start(), calls=%async_computation.6 | async-start | bytes 2211840 | tf_op jit(solution)/shard_map/while/body/eval_jaxpr/all_gather | solution.py:151
  392.7 82.7 %reduce-scatter.9.cloned.1.call-start = ((), (), s32[]{:S(2)}) async-start(), calls=%async_computation.8 | async-start | bytes 2211840 | tf_op jit(solution)/shard_map/while/body/eval_jaxpr/reduce_scatter | solution.py:173
  442.8 79.6 %all-gather.5.cloned.1.call-start = ((), (), s32[]{:S(2)}) async-start(), calls=%async_computation.9 | async-start | bytes 2211840 | tf_op jit(solution)/shard_map/while/body/eval_jaxpr/all_gather | solution.py:188
  489.8 88.6 %reduce-scatter.7.cloned.1.call-start = ((), (), s32[]{:S(2)}) async-start(), calls=%async_computation.7 | async-start | bytes 2211840 | tf_op jit(solution)/shard_map/while/body/eval_jaxpr/reduce_scatter | solution.py:159
  503.1 90.2 %reduce-scatter.11.cloned.1.call-start = ((), (), s32[]{:S(2)}) async-start(), calls=%async_computation.10 | async-start | bytes 2211840 | tf_op jit(solution)/shard_map/while/body/eval_jaxpr/reduce_scatter | solution.py:224
  568.1 9.0 copy-start.25
  584.6 19.5 %copy-start.30 = (f32[288]{0:T(512)S(1)}, f32[288]{0:T(512)}, u32[]{:S(2)}) copy-start(f32[288]{0:T(512)} %get-tuple-element.1286) | copy-start | bytes 3460 | tf_op jit(solution)/shard_map/while
  584.6 19.5 %copy-start.33 = (f32[288]{0:T(512)S(1)}, f32[288]{0:T(512)}, u32[]{:S(2)}) copy-start(f32[288]{0:T(512)} %get-tuple-element.1285) | copy-start | bytes 3460 | tf_op jit(solution)/shard_map/while
  593.3 13.4 copy-start.19
  593.3 13.4 copy-start.21
  593.3 13.4 copy-start.40
  593.4 13.4 copy-start.42
  607.0 9.8 copy-start.41
  607.0 163.9 %copy-start.18 = (f32[1152]{0:T(1024)}, f32[1152]{0:T(1024)S(1)}, u32[]{:S(2)}) copy-start(f32[1152]{0:T(1024)S(1)} %get-tuple-element.1334) | copy-start | bytes 13828 | tf_op jit(solution)/shard_map/while
  607.0 55.1 %reduce-scatter.5.cloned.1.call-start = ((), (), s32[]{:S(2)}) async-start(), calls=%async_computation.5 | async-start | bytes 2211840 | tf_op jit(solution)/shard_map/while/body/eval_jaxpr/reduce_scatter | solution.py:137
  608.9 165.5 %copy-start.15 = (f32[729]{0:T(1024)}, f32[729]{0:T(1024)S(1)}, u32[]{:S(2)}) copy-start(f32[729]{0:T(1024)S(1)} %broadcast_multiply_fusion.11) | copy-start | bytes 8752 | tf_op jit(solution)/shard_map/while
  629.5 76.9 %all-gather.3.cloned.1.call-start = ((), (), s32[]{:S(2)}) async-start(), calls=%async_computation.6 | async-start | bytes 2211840 | tf_op jit(solution)/shard_map/while/body/eval_jaxpr/all_gather | solution.py:151
  673.8 82.7 %reduce-scatter.9.cloned.1.call-start = ((), (), s32[]{:S(2)}) async-start(), calls=%async_computation.8 | async-start | bytes 2211840 | tf_op jit(solution)/shard_map/while/body/eval_jaxpr/reduce_scatter | solution.py:173
  723.9 79.6 %all-gather.5.cloned.1.call-start = ((), (), s32[]{:S(2)}) async-start(), calls=%async_computation.9 | async-start | bytes 2211840 | tf_op jit(solution)/shard_map/while/body/eval_jaxpr/all_gather | solution.py:188
  770.8 88.4 %reduce-scatter.7.cloned.1.call-start = ((), (), s32[]{:S(2)}) async-start(), calls=%async_computation.7 | async-start | bytes 2211840 | tf_op jit(solution)/shard_map/while/body/eval_jaxpr/reduce_scatter | solution.py:159
  784.1 90.1 %reduce-scatter.11.cloned.1.call-start = ((), (), s32[]{:S(2)}) async-start(), calls=%async_computation.10 | async-start | bytes 2211840 | tf_op jit(solution)/shard_map/while/body/eval_jaxpr/reduce_scatter | solution.py:224
  865.5 19.6 %copy-start.30 = (f32[288]{0:T(512)S(1)}, f32[288]{0:T(512)}, u32[]{:S(2)}) copy-start(f32[288]{0:T(512)} %get-tuple-element.1286) | copy-start | bytes 3460 | tf_op jit(solution)/shard_map/while
  865.5 19.6 %copy-start.33 = (f32[288]{0:T(512)S(1)}, f32[288]{0:T(512)}, u32[]{:S(2)}) copy-start(f32[288]{0:T(512)} %get-tuple-element.1285) | copy-start | bytes 3460 | tf_op jit(solution)/shard_map/while
  874.2 13.4 copy-start.19
  874.2 13.4 copy-start.21
  874.2 13.4 copy-start.40
  874.2 13.4 copy-start.42
  888.1 9.8 copy-start.41
  888.1 163.9 %copy-start.18 = (f32[1152]{0:T(1024)}, f32[1152]{0:T(1024)S(1)}, u32[]{:S(2)}) copy-start(f32[1152]{0:T(1024)S(1)} %get-tuple-element.1334) | copy-start | bytes 13828 | tf_op jit(solution)/shard_map/while
  888.1 55.1 %reduce-scatter.5.cloned.1.call-start = ((), (), s32[]{:S(2)}) async-start(), calls=%async_computation.5 | async-start | bytes 2211840 | tf_op jit(solution)/shard_map/while/body/eval_jaxpr/reduce_scatter | solution.py:137
  890.0 165.5 %copy-start.15 = (f32[729]{0:T(1024)}, f32[729]{0:T(1024)S(1)}, u32[]{:S(2)}) copy-start(f32[729]{0:T(1024)S(1)} %broadcast_multiply_fusion.11) | copy-start | bytes 8752 | tf_op jit(solution)/shard_map/while
  910.6 76.9 %all-gather.3.cloned.1.call-start = ((), (), s32[]{:S(2)}) async-start(), calls=%async_computation.6 | async-start | bytes 2211840 | tf_op jit(solution)/shard_map/while/body/eval_jaxpr/all_gather | solution.py:151
  954.9 82.7 %reduce-scatter.9.cloned.1.call-start = ((), (), s32[]{:S(2)}) async-start(), calls=%async_computation.8 | async-start | bytes 2211840 | tf_op jit(solution)/shard_map/while/body/eval_jaxpr/reduce_scatter | solution.py:173
  1005.0 79.6 %all-gather.5.cloned.1.call-start = ((), (), s32[]{:S(2)}) async-start(), calls=%async_computation.9 | async-start | bytes 2211840 | tf_op jit(solution)/shard_map/while/body/eval_jaxpr/all_gather | solution.py:188
  1051.9 88.6 %reduce-scatter.7.cloned.1.call-start = ((), (), s32[]{:S(2)}) async-start(), calls=%async_computation.7 | async-start | bytes 2211840 | tf_op jit(solution)/shard_map/while/body/eval_jaxpr/reduce_scatter | solution.py:159
  1065.2 90.2 %reduce-scatter.11.cloned.1.call-start = ((), (), s32[]{:S(2)}) async-start(), calls=%async_computation.10 | async-start | bytes 2211840 | tf_op jit(solution)/shard_map/while/body/eval_jaxpr/reduce_scatter | solution.py:224
  1130.2 9.0 copy-start.25
  1146.8 19.5 %copy-start.30 = (f32[288]{0:T(512)S(1)}, f32[288]{0:T(512)}, u32[]{:S(2)}) copy-start(f32[288]{0:T(512)} %get-tuple-element.1286) | copy-start | bytes 3460 | tf_op jit(solution)/shard_map/while
  1146.8 19.5 %copy-start.33 = (f32[288]{0:T(512)S(1)}, f32[288]{0:T(512)}, u32[]{:S(2)}) copy-start(f32[288]{0:T(512)} %get-tuple-element.1285) | copy-start | bytes 3460 | tf_op jit(solution)/shard_map/while
  1155.5 13.4 copy-start.19
  1155.5 13.4 copy-start.21
  1155.5 13.4 copy-start.40
  1155.5 13.4 copy-start.42
  1171.6 172.7 %all-reduce.13.cloned.1.call-start = ((), (), s32[]{:S(2)}) async-start(), calls=%async_computation.4 | async-start | bytes 15261696 | tf_op jit(solution)/shard_map/psum | solution.py:293
  (132 other events, 667.1 us)
Sparse Core Ops, SparseCore 0:
  64.7 35.1 reduce-scatter.4
  111.8 32.4 all-gather.2
  161.9 32.4 reduce-scatter.8
  208.8 32.4 all-gather.4
  244.2 32.4 reduce-scatter.6
  279.6 32.4 reduce-scatter.10
  348.6 32.4 reduce-scatter.4
  392.9 32.4 all-gather.2
  443.0 32.4 reduce-scatter.8
  489.9 32.4 all-gather.4
  525.4 32.4 reduce-scatter.6
  560.8 32.4 reduce-scatter.10
  629.6 32.4 reduce-scatter.4
  673.9 32.4 all-gather.2
  724.0 32.4 reduce-scatter.8
  770.9 32.4 all-gather.4
  806.3 32.4 reduce-scatter.6
  841.7 32.4 reduce-scatter.10
  910.7 32.4 reduce-scatter.4
  955.0 32.4 all-gather.2
  1005.1 32.4 reduce-scatter.8
  1052.0 32.4 all-gather.4
  1087.6 32.4 reduce-scatter.6
  1123.0 32.4 reduce-scatter.10
Sparse Core Ops, SparseCore 1:
  1182.1 162.1 all-reduce.12
where the time goes:
time: 1370 us; the launch traced here: 1360 us
  waiting for transfers between devices  569 us (42%)
  matrix products  335 us (24%)
  other arithmetic  226 us (16%)
  blocking collectives  137 us (10%)
  local copies, waits for them, and re-layouts  69.1 us (5%)
  between operations  15.9 us (1%)
    psum x1, waiting for transfers between devices, local(): lax.psum(grad_qkv.astype(jnp.bfloat16), 'dp').astype(jnp.float32)  128 us
    all_gather x4, waiting for transfers between devices, layer_step(): normed_two = lax.all_gather(own_normed, 'tensor', axis=1, tiled=True)  126 us
    reduce_scatter x4, waiting for transfers between devices, layer_step(): lax.psum_scatter(back_mlp.astype(jnp.bfloat16), 'tensor', scatter_dimensi...  116 us
    reduce_scatter x4, waiting for transfers between devices, layer_step(): lax.psum_scatter(partial_out, 'tensor', scatter_dimension=1, tiled=True)  110 us
    psum x12, blocking collectives, group_stats(): return lax.psum((first, second), 'tensor')  109 us
    all_gather x4, waiting for transfers between devices, layer_step(): lax.all_gather(d_residual.astype(jnp.bfloat16), 'tensor', axis=1, tiled=T...  77.6 us
    dot_general x12, matrix products, contract_rows(): lax.dot_general(left, right, (((0,), (0,)), ((), ())), preferred_element_...  67.7 us
    dot_general x12, matrix products, contract_cols(): lax.dot_general(left, right, (((1,), (1,)), ((), ())), preferred_element_...  55.6 us
  transfers between devices with their start and end apart: 25, of which 21 were waited for; matrix products, arithmetic and copies ran while one was open for 26% of the time, Pallas kernels for 0%

commit v1 on v0

--- a/solution.py
+++ b/solution.py
@@ -287,10 +287,14 @@
         grad_fc2_w,
         grad_fc2_b,
     ) = grads
+
+    def _track_tiles(vals):
+        return jnp.sum(jax.lax.all_gather(vals, "dp"), axis=0)
+
     summed = (
         lax.psum(grad_gain_one.astype(jnp.bfloat16), "dp").astype(jnp.float32),
         lax.psum(grad_shift_one.astype(jnp.bfloat16), "dp").astype(jnp.float32),
-        lax.psum(grad_qkv.astype(jnp.bfloat16), "dp").astype(jnp.float32),
+        _track_tiles(grad_qkv.astype(jnp.bfloat16)).astype(jnp.float32),
         lax.psum(grad_qv.astype(jnp.bfloat16), "dp").astype(jnp.float32),
         lax.psum(grad_out_w.astype(jnp.bfloat16), "dp").astype(jnp.float32),
         lax.psum(grad_out_b.astype(jnp.bfloat16), "dp").astype(jnp.float32),

time: 1370 us -> 1480 us (1.080)
  waiting for transfers between devices: 569 us -> 664 us
    all_gather x0 -> x1, waiting for transfers between devices: none -> 136 us  [_track_tiles(): return jnp.sum(jax.lax.all_gather(vals, 'dp'), axis=0)]
    psum x1, waiting for transfers between devices: 128 us -> 86.5 us  [local(): lax.psum(grad_out_w.astype(jnp.bfloat16), 'dp').astype(jnp.float32)]
  transfers between devices with their start and end apart: 25 -> 26, of which waited for: 21 -> 22; matrix products, arithmetic and copies ran while one was open for 26% -> 25% of each run, Pallas kernels for 0% -> 0%
where the time goes in v1:
time: 1480 us; the launch traced here: 1470 us
  waiting for transfers between devices  664 us (45%)
  matrix products  334 us (23%)
  other arithmetic  238 us (16%)
  blocking collectives  137 us (9%)
  local copies, waits for them, and re-layouts  68.6 us (5%)
  between operations  15.9 us (1%)
    all_gather x1, waiting for transfers between devices, _track_tiles(): return jnp.sum(jax.lax.all_gather(vals, 'dp'), axis=0)  136 us
    all_gather x4, waiting for transfers between devices, layer_step(): normed_two = lax.all_gather(own_normed, 'tensor', axis=1, tiled=True)  126 us
    reduce_scatter x4, waiting for transfers between devices, layer_step(): lax.psum_scatter(back_mlp.astype(jnp.bfloat16), 'tensor', scatter_dimensi...  116 us
    reduce_scatter x4, waiting for transfers between devices, layer_step(): lax.psum_scatter(partial_out, 'tensor', scatter_dimension=1, tiled=True)  110 us
    psum x12, blocking collectives, group_stats(): return lax.psum((first, second), 'tensor')  109 us
    psum x1, waiting for transfers between devices, local(): lax.psum(grad_out_w.astype(jnp.bfloat16), 'dp').astype(jnp.float32)  86.5 us
    all_gather x4, waiting for transfers between devices, layer_step(): lax.all_gather(d_residual.astype(jnp.bfloat16), 'tensor', axis=1, tiled=T...  77.5 us
    dot_general x12, matrix products, contract_rows(): lax.dot_general(left, right, (((0,), (0,)), ((), ())), preferred_element_...  67.7 us
  transfers between devices with their start and end apart: 26, of which 22 were waited for; matrix products, arithmetic and copies ran while one was open for 25% of the time, Pallas kernels for 0%

profile of v1, /device:TPU:0, one launch (start us, length us, event | category | flops | bytes accessed | tf_op | source)
XLA Modules:
  0.0 1469.7 jit_solution(3503463476990974221)
XLA Ops:
  16.7 12.7 copy.41
  29.4 12.7 copy.42
  42.1 1129.9 %while.42 = (s32[]{:T(128)}, f32[4,729,288]{1,2,0:T(8,128)}, f32[4,729,288]{1,2,0:T(8,128)}, f32[288]{0:T(512)}, f32[288]{0:T(512)}, /*index=5*/f32[3,1152,288]{...) while((s32[]{:T(128)}, f32[4,729,288]{1,2,0:T(8,128)}, ...), condition=%wide.region_30.31_spmd.clone, body=%wide.region_0.30_spmd.clone.sunk | while | flops 18614964224 | bytes 394633504 | solution.py:273
  70.5 29.5 %reduce-scatter.5.cloned.1.call-done = bf16[729,288]{0,1:T(8,128)(2,1)} async-done(((bf16[729,1152]{0,1:T(8,128)(2,1)}), bf16[729,288]{0,1:T(8,128)(2,1)}) %reduce-scatter.5.cloned.1.call-update) | async-done | bytes 419920 | tf_op jit(solution)/shard_map/while/body/eval_jaxpr/reduce_scatter | solution.py:137
  101.5 9.1 all-reduce.8
  112.9 31.3 %all-gather.7.cloned.1.call-done = bf16[729,1152]{0,1:T(8,128)(2,1)} async-done(((bf16[729,288]{0,1:T(8,128)(2,1)}), bf16[729,1152]{0,1:T(8,128)(2,1)}) %all-gather.7.cloned.1.call-update) | async-done | bytes 1679632 | tf_op jit(solution)/shard_map/while/body/eval_jaxpr/all_gather | solution.py:151
  148.9 7.7 convert_reduce_fusion.11
  165.3 29.0 %reduce-scatter.9.cloned.1.call-done = bf16[729,288]{0,1:T(8,128)(2,1)} async-done(((bf16[729,1152]{0,1:T(8,128)(2,1)}), bf16[729,288]{0,1:T(8,128)(2,1)}) %reduce-scatter.9.cloned.1.call-update) | async-done | bytes 419920 | tf_op jit(solution)/shard_map/while/body/eval_jaxpr/reduce_scatter | solution.py:173
  196.3 9.1 all-reduce.9
  215.2 6.1 convolution_convert_fusion.17
  221.4 19.9 %all-gather.9.cloned.1.call-done = bf16[729,1152]{0,1:T(8,128)(2,1)} async-done(((bf16[729,288]{0,1:T(8,128)(2,1)}), bf16[729,1152]{0,1:T(8,128)(2,1)}) %all-gather.9.cloned.1.call-update) | async-done | bytes 1679632 | tf_op jit(solution)/shard_map/while/body/eval_jaxpr/all_gather | solution.py:188
  243.6 7.6 multiply_reduce_fusion.9
  251.2 10.4 multiply_convert_fusion.9
  278.1 6.8 convolution_add_fusion.12
  285.5 6.8 convolution_add_fusion.13
  299.2 6.0 bitcast_add_fusion.3
  305.1 6.9 reduce-scatter.11.cloned.1.call-done
  313.7 9.1 all-reduce.10
  354.3 26.8 %reduce-scatter.5.cloned.1.call-done = bf16[729,288]{0,1:T(8,128)(2,1)} async-done(((bf16[729,1152]{0,1:T(8,128)(2,1)}), bf16[729,288]{0,1:T(8,128)(2,1)}) %reduce-scatter.5.cloned.1.call-update) | async-done | bytes 419920 | tf_op jit(solution)/shard_map/while/body/eval_jaxpr/reduce_scatter | solution.py:137
  382.6 9.1 all-reduce.8
  393.6 31.7 %all-gather.7.cloned.1.call-done = bf16[729,1152]{0,1:T(8,128)(2,1)} async-done(((bf16[729,288]{0,1:T(8,128)(2,1)}), bf16[729,1152]{0,1:T(8,128)(2,1)}) %all-gather.7.cloned.1.call-update) | async-done | bytes 1679632 | tf_op jit(solution)/shard_map/while/body/eval_jaxpr/all_gather | solution.py:151
  430.0 7.7 convert_reduce_fusion.11
  446.4 29.0 %reduce-scatter.9.cloned.1.call-done = bf16[729,288]{0,1:T(8,128)(2,1)} async-done(((bf16[729,1152]{0,1:T(8,128)(2,1)}), bf16[729,288]{0,1:T(8,128)(2,1)}) %reduce-scatter.9.cloned.1.call-update) | async-done | bytes 419920 | tf_op jit(solution)/shard_map/while/body/eval_jaxpr/reduce_scatter | solution.py:173
  477.4 9.1 all-reduce.9
  496.9 6.1 convolution_convert_fusion.17
  503.1 19.2 %all-gather.9.cloned.1.call-done = bf16[729,1152]{0,1:T(8,128)(2,1)} async-done(((bf16[729,288]{0,1:T(8,128)(2,1)}), bf16[729,1152]{0,1:T(8,128)(2,1)}) %all-gather.9.cloned.1.call-update) | async-done | bytes 1679632 | tf_op jit(solution)/shard_map/while/body/eval_jaxpr/all_gather | solution.py:188
  524.7 7.6 multiply_reduce_fusion.9
  532.3 10.3 multiply_convert_fusion.9
  559.2 8.2 convolution_add_fusion.12
  568.1 8.4 convolution_add_fusion.13
  584.6 7.2 bitcast_add_fusion.3
  595.0 9.1 all-reduce.10
  635.3 26.8 %reduce-scatter.5.cloned.1.call-done = bf16[729,288]{0,1:T(8,128)(2,1)} async-done(((bf16[729,1152]{0,1:T(8,128)(2,1)}), bf16[729,288]{0,1:T(8,128)(2,1)}) %reduce-scatter.5.cloned.1.call-update) | async-done | bytes 419920 | tf_op jit(solution)/shard_map/while/body/eval_jaxpr/reduce_scatter | solution.py:137
  663.6 9.1 all-reduce.8
  674.8 31.5 %all-gather.7.cloned.1.call-done = bf16[729,1152]{0,1:T(8,128)(2,1)} async-done(((bf16[729,288]{0,1:T(8,128)(2,1)}), bf16[729,1152]{0,1:T(8,128)(2,1)}) %all-gather.7.cloned.1.call-update) | async-done | bytes 1679632 | tf_op jit(solution)/shard_map/while/body/eval_jaxpr/all_gather | solution.py:151
  711.0 7.7 convert_reduce_fusion.11
  727.4 29.0 %reduce-scatter.9.cloned.1.call-done = bf16[729,288]{0,1:T(8,128)(2,1)} async-done(((bf16[729,1152]{0,1:T(8,128)(2,1)}), bf16[729,288]{0,1:T(8,128)(2,1)}) %reduce-scatter.9.cloned.1.call-update) | async-done | bytes 419920 | tf_op jit(solution)/shard_map/while/body/eval_jaxpr/reduce_scatter | solution.py:173
  758.4 9.1 all-reduce.9
  777.9 6.1 convolution_convert_fusion.17
  784.1 19.2 %all-gather.9.cloned.1.call-done = bf16[729,1152]{0,1:T(8,128)(2,1)} async-done(((bf16[729,288]{0,1:T(8,128)(2,1)}), bf16[729,1152]{0,1:T(8,128)(2,1)}) %all-gather.9.cloned.1.call-update) | async-done | bytes 1679632 | tf_op jit(solution)/shard_map/while/body/eval_jaxpr/all_gather | solution.py:188
  805.7 7.6 multiply_reduce_fusion.9
  813.3 10.4 multiply_convert_fusion.9
  840.2 8.2 convolution_add_fusion.12
  849.1 8.2 convolution_add_fusion.13
  865.4 7.2 bitcast_add_fusion.3
  875.8 9.1 all-reduce.10
  916.4 26.8 %reduce-scatter.5.cloned.1.call-done = bf16[729,288]{0,1:T(8,128)(2,1)} async-done(((bf16[729,1152]{0,1:T(8,128)(2,1)}), bf16[729,288]{0,1:T(8,128)(2,1)}) %reduce-scatter.5.cloned.1.call-update) | async-done | bytes 419920 | tf_op jit(solution)/shard_map/while/body/eval_jaxpr/reduce_scatter | solution.py:137
  944.7 9.1 all-reduce.8
  955.6 31.7 %all-gather.7.cloned.1.call-done = bf16[729,1152]{0,1:T(8,128)(2,1)} async-done(((bf16[729,288]{0,1:T(8,128)(2,1)}), bf16[729,1152]{0,1:T(8,128)(2,1)}) %all-gather.7.cloned.1.call-update) | async-done | bytes 1679632 | tf_op jit(solution)/shard_map/while/body/eval_jaxpr/all_gather | solution.py:151
  992.1 7.7 convert_reduce_fusion.11
  1008.5 29.0 %reduce-scatter.9.cloned.1.call-done = bf16[729,288]{0,1:T(8,128)(2,1)} async-done(((bf16[729,1152]{0,1:T(8,128)(2,1)}), bf16[729,288]{0,1:T(8,128)(2,1)}) %reduce-scatter.9.cloned.1.call-update) | async-done | bytes 419920 | tf_op jit(solution)/shard_map/while/body/eval_jaxpr/reduce_scatter | solution.py:173
  1039.5 9.0 all-reduce.9
  1059.0 6.1 convolution_convert_fusion.17
  1065.2 19.2 %all-gather.9.cloned.1.call-done = bf16[729,1152]{0,1:T(8,128)(2,1)} async-done(((bf16[729,288]{0,1:T(8,128)(2,1)}), bf16[729,1152]{0,1:T(8,128)(2,1)}) %all-gather.9.cloned.1.call-update) | async-done | bytes 1679632 | tf_op jit(solution)/shard_map/while/body/eval_jaxpr/all_gather | solution.py:188
  1086.8 7.6 multiply_reduce_fusion.9
  1094.4 10.3 multiply_convert_fusion.9
  1121.3 8.2 convolution_add_fusion.12
  1130.2 8.4 convolution_add_fusion.13
  1146.7 7.2 bitcast_add_fusion.3
  1157.1 9.1 all-reduce.10
  1186.2 28.1 %all-reduce.3 = (bf16[288]{0:T(512)(128)(2,1)S(1)}, bf16[288]{0:T(512)(128)(2,1)S(1)}, bf16[2,288]{1,0:T(2,128)(2,1)S(1)}, bf16[288]{0:T(512)(128)(2,1)S(1)}, bf...) all-reduce(bf16[288]{0:T(512)(128)(2,1)S(1)} %convert_element_type., ...), channel_id=1, replica_groups=mesh['tensor'=4,'dp'=8] {'dp'}, use_global_device_ids=true, to_apply=%region_31.32 | all-reduce | flops 3380 | bytes 13520 | tf_op jit(solution)/shard_map/psum | solution.py:295
  1219.0 86.5 %all-reduce.13.cloned.1.call-done = (bf16[288,1152]{1,0:T(8,128)(2,1)}, bf16[1152,1076]{0,1:T(8,128)(2,1)}, bf16[1076,1152]{1,0:T(8,128)(2,1)}) async-done(((bf16[288,1152]{1,0:T(8,128)(2,1)}, bf16[1152,1076]{0,1:T(8,128)(2,1)}, bf16[1076,1152]{1,0:T(8,128)(2,1)}), (bf16[288,1152]{1,0:T(8,128)(2,1)}, bf16[1152,1076]{0,1:T(8,128)(2,1)}, bf16[1076,1152]{1,0:T(8,128)(2,1)})) %all-reduce.13.cloned.1.call-update) | async-done | bytes 5621776 | tf_op jit(solution)/shard_map/psum | solution.py:299
  1314.8 135.8 %all-gather.5.cloned.1.call-done = bf16[24,1152,288]{1,2,0:T(8,128)(2,1)} async-done(((bf16[3,1152,288]{1,2,0:T(8,128)(2,1)}), bf16[24,1152,288]{1,2,0:T(8,128)(2,1)}) %all-gather.5.cloned.1.call-update) | async-done | bytes 15925264 | tf_op jit(solution)/shard_map/all_gather | solution.py:292
  1450.7 9.2 reduce_sum.300
  (635 shorter events, 396.3 us)
Async XLA Ops:
  42.1 9.8 copy-start.39
  42.1 166.6 %copy-start.16 = (f32[1152]{0:T(1024)}, f32[1152]{0:T(1024)S(1)}, u32[]{:S(2)}) copy-start(f32[1152]{0:T(1024)S(1)} %get-tuple-element.1364) | copy-start | bytes 13828 | tf_op jit(solution)/shard_map/while
  42.1 57.8 %reduce-scatter.5.cloned.1.call-start = ((), (), s32[]{:S(2)}) async-start(), calls=%async_computation.6 | async-start | bytes 2211840 | tf_op jit(solution)/shard_map/while/body/eval_jaxpr/reduce_scatter | solution.py:137
  44.0 167.6 %copy-start.13 = (f32[729]{0:T(1024)}, f32[729]{0:T(1024)S(1)}, u32[]{:S(2)}) copy-start(f32[729]{0:T(1024)S(1)} %broadcast_multiply_fusion.11) | copy-start | bytes 8752 | tf_op jit(solution)/shard_map/while
  64.6 79.6 %all-gather.7.cloned.1.call-start = ((), (), s32[]{:S(2)}) async-start(), calls=%async_computation.7 | async-start | bytes 2211840 | tf_op jit(solution)/shard_map/while/body/eval_jaxpr/all_gather | solution.py:151
  111.6 82.7 %reduce-scatter.9.cloned.1.call-start = ((), (), s32[]{:S(2)}) async-start(), calls=%async_computation.9 | async-start | bytes 2211840 | tf_op jit(solution)/shard_map/while/body/eval_jaxpr/reduce_scatter | solution.py:173
  161.7 79.5 %all-gather.9.cloned.1.call-start = ((), (), s32[]{:S(2)}) async-start(), calls=%async_computation.10 | async-start | bytes 2211840 | tf_op jit(solution)/shard_map/while/body/eval_jaxpr/all_gather | solution.py:188
  208.6 84.9 %reduce-scatter.7.cloned.1.call-start = ((), (), s32[]{:S(2)}) async-start(), calls=%async_computation.8 | async-start | bytes 2211840 | tf_op jit(solution)/shard_map/while/body/eval_jaxpr/reduce_scatter | solution.py:159
  221.3 90.7 %reduce-scatter.11.cloned.1.call-start = ((), (), s32[]{:S(2)}) async-start(), calls=%async_computation.11 | async-start | bytes 2211840 | tf_op jit(solution)/shard_map/while/body/eval_jaxpr/reduce_scatter | solution.py:224
  299.1 12.9 copy-start.15
  299.2 23.7 %copy-start.28 = (f32[288]{0:T(512)S(1)}, f32[288]{0:T(512)}, u32[]{:S(2)}) copy-start(f32[288]{0:T(512)} %get-tuple-element.1316) | copy-start | bytes 3460 | tf_op jit(solution)/shard_map/while
  299.2 23.7 %copy-start.31 = (f32[288]{0:T(512)S(1)}, f32[288]{0:T(512)}, u32[]{:S(2)}) copy-start(f32[288]{0:T(512)} %get-tuple-element.1315) | copy-start | bytes 3460 | tf_op jit(solution)/shard_map/while
  312.0 13.4 copy-start.17
  312.0 13.4 copy-start.19
  312.0 13.4 copy-start.38
  312.0 13.4 copy-start.40
  325.9 9.8 copy-start.39
  325.9 163.9 %copy-start.16 = (f32[1152]{0:T(1024)}, f32[1152]{0:T(1024)S(1)}, u32[]{:S(2)}) copy-start(f32[1152]{0:T(1024)S(1)} %get-tuple-element.1364) | copy-start | bytes 13828 | tf_op jit(solution)/shard_map/while
  325.9 55.1 %reduce-scatter.5.cloned.1.call-start = ((), (), s32[]{:S(2)}) async-start(), calls=%async_computation.6 | async-start | bytes 2211840 | tf_op jit(solution)/shard_map/while/body/eval_jaxpr/reduce_scatter | solution.py:137
  327.8 165.5 %copy-start.13 = (f32[729]{0:T(1024)}, f32[729]{0:T(1024)S(1)}, u32[]{:S(2)}) copy-start(f32[729]{0:T(1024)S(1)} %broadcast_multiply_fusion.11) | copy-start | bytes 8752 | tf_op jit(solution)/shard_map/while
  348.4 76.9 %all-gather.7.cloned.1.call-start = ((), (), s32[]{:S(2)}) async-start(), calls=%async_computation.7 | async-start | bytes 2211840 | tf_op jit(solution)/shard_map/while/body/eval_jaxpr/all_gather | solution.py:151
  392.7 82.7 %reduce-scatter.9.cloned.1.call-start = ((), (), s32[]{:S(2)}) async-start(), calls=%async_computation.9 | async-start | bytes 2211840 | tf_op jit(solution)/shard_map/while/body/eval_jaxpr/reduce_scatter | solution.py:173
  442.8 79.5 %all-gather.9.cloned.1.call-start = ((), (), s32[]{:S(2)}) async-start(), calls=%async_computation.10 | async-start | bytes 2211840 | tf_op jit(solution)/shard_map/while/body/eval_jaxpr/all_gather | solution.py:188
  489.7 88.6 %reduce-scatter.7.cloned.1.call-start = ((), (), s32[]{:S(2)}) async-start(), calls=%async_computation.8 | async-start | bytes 2211840 | tf_op jit(solution)/shard_map/while/body/eval_jaxpr/reduce_scatter | solution.py:159
  503.1 90.2 %reduce-scatter.11.cloned.1.call-start = ((), (), s32[]{:S(2)}) async-start(), calls=%async_computation.11 | async-start | bytes 2211840 | tf_op jit(solution)/shard_map/while/body/eval_jaxpr/reduce_scatter | solution.py:224
  568.1 9.0 copy-start.23
  584.6 19.5 %copy-start.28 = (f32[288]{0:T(512)S(1)}, f32[288]{0:T(512)}, u32[]{:S(2)}) copy-start(f32[288]{0:T(512)} %get-tuple-element.1316) | copy-start | bytes 3460 | tf_op jit(solution)/shard_map/while
  584.6 19.5 %copy-start.31 = (f32[288]{0:T(512)S(1)}, f32[288]{0:T(512)}, u32[]{:S(2)}) copy-start(f32[288]{0:T(512)} %get-tuple-element.1315) | copy-start | bytes 3460 | tf_op jit(solution)/shard_map/while
  593.3 13.4 copy-start.17
  593.3 13.4 copy-start.19
  593.3 13.4 copy-start.38
  593.3 13.4 copy-start.40
  606.9 9.8 copy-start.39
  606.9 163.9 %copy-start.16 = (f32[1152]{0:T(1024)}, f32[1152]{0:T(1024)S(1)}, u32[]{:S(2)}) copy-start(f32[1152]{0:T(1024)S(1)} %get-tuple-element.1364) | copy-start | bytes 13828 | tf_op jit(solution)/shard_map/while
  606.9 55.1 %reduce-scatter.5.cloned.1.call-start = ((), (), s32[]{:S(2)}) async-start(), calls=%async_computation.6 | async-start | bytes 2211840 | tf_op jit(solution)/shard_map/while/body/eval_jaxpr/reduce_scatter | solution.py:137
  608.8 165.5 %copy-start.13 = (f32[729]{0:T(1024)}, f32[729]{0:T(1024)S(1)}, u32[]{:S(2)}) copy-start(f32[729]{0:T(1024)S(1)} %broadcast_multiply_fusion.11) | copy-start | bytes 8752 | tf_op jit(solution)/shard_map/while
  629.4 76.9 %all-gather.7.cloned.1.call-start = ((), (), s32[]{:S(2)}) async-start(), calls=%async_computation.7 | async-start | bytes 2211840 | tf_op jit(solution)/shard_map/while/body/eval_jaxpr/all_gather | solution.py:151
  673.7 82.7 %reduce-scatter.9.cloned.1.call-start = ((), (), s32[]{:S(2)}) async-start(), calls=%async_computation.9 | async-start | bytes 2211840 | tf_op jit(solution)/shard_map/while/body/eval_jaxpr/reduce_scatter | solution.py:173
  723.8 79.5 %all-gather.9.cloned.1.call-start = ((), (), s32[]{:S(2)}) async-start(), calls=%async_computation.10 | async-start | bytes 2211840 | tf_op jit(solution)/shard_map/while/body/eval_jaxpr/all_gather | solution.py:188
  770.7 88.5 %reduce-scatter.7.cloned.1.call-start = ((), (), s32[]{:S(2)}) async-start(), calls=%async_computation.8 | async-start | bytes 2211840 | tf_op jit(solution)/shard_map/while/body/eval_jaxpr/reduce_scatter | solution.py:159
  784.1 90.0 %reduce-scatter.11.cloned.1.call-start = ((), (), s32[]{:S(2)}) async-start(), calls=%async_computation.11 | async-start | bytes 2211840 | tf_op jit(solution)/shard_map/while/body/eval_jaxpr/reduce_scatter | solution.py:224
  865.4 19.5 %copy-start.28 = (f32[288]{0:T(512)S(1)}, f32[288]{0:T(512)}, u32[]{:S(2)}) copy-start(f32[288]{0:T(512)} %get-tuple-element.1316) | copy-start | bytes 3460 | tf_op jit(solution)/shard_map/while
  865.4 19.5 %copy-start.31 = (f32[288]{0:T(512)S(1)}, f32[288]{0:T(512)}, u32[]{:S(2)}) copy-start(f32[288]{0:T(512)} %get-tuple-element.1315) | copy-start | bytes 3460 | tf_op jit(solution)/shard_map/while
  874.1 13.4 copy-start.17
  874.1 13.4 copy-start.19
  874.1 13.4 copy-start.38
  874.1 13.4 copy-start.40
  888.0 9.8 copy-start.39
  888.0 163.9 %copy-start.16 = (f32[1152]{0:T(1024)}, f32[1152]{0:T(1024)S(1)}, u32[]{:S(2)}) copy-start(f32[1152]{0:T(1024)S(1)} %get-tuple-element.1364) | copy-start | bytes 13828 | tf_op jit(solution)/shard_map/while
  888.0 55.1 %reduce-scatter.5.cloned.1.call-start = ((), (), s32[]{:S(2)}) async-start(), calls=%async_computation.6 | async-start | bytes 2211840 | tf_op jit(solution)/shard_map/while/body/eval_jaxpr/reduce_scatter | solution.py:137
  889.9 165.5 %copy-start.13 = (f32[729]{0:T(1024)}, f32[729]{0:T(1024)S(1)}, u32[]{:S(2)}) copy-start(f32[729]{0:T(1024)S(1)} %broadcast_multiply_fusion.11) | copy-start | bytes 8752 | tf_op jit(solution)/shard_map/while
  910.5 76.9 %all-gather.7.cloned.1.call-start = ((), (), s32[]{:S(2)}) async-start(), calls=%async_computation.7 | async-start | bytes 2211840 | tf_op jit(solution)/shard_map/while/body/eval_jaxpr/all_gather | solution.py:151
  954.8 82.7 %reduce-scatter.9.cloned.1.call-start = ((), (), s32[]{:S(2)}) async-start(), calls=%async_computation.9 | async-start | bytes 2211840 | tf_op jit(solution)/shard_map/while/body/eval_jaxpr/reduce_scatter | solution.py:173
  1004.9 79.5 %all-gather.9.cloned.1.call-start = ((), (), s32[]{:S(2)}) async-start(), calls=%async_computation.10 | async-start | bytes 2211840 | tf_op jit(solution)/shard_map/while/body/eval_jaxpr/all_gather | solution.py:188
  1051.8 88.7 %reduce-scatter.7.cloned.1.call-start = ((), (), s32[]{:S(2)}) async-start(), calls=%async_computation.8 | async-start | bytes 2211840 | tf_op jit(solution)/shard_map/while/body/eval_jaxpr/reduce_scatter | solution.py:159
  1065.1 90.2 %reduce-scatter.11.cloned.1.call-start = ((), (), s32[]{:S(2)}) async-start(), calls=%async_computation.11 | async-start | bytes 2211840 | tf_op jit(solution)/shard_map/while/body/eval_jaxpr/reduce_scatter | solution.py:224
  1146.7 19.5 %copy-start.28 = (f32[288]{0:T(512)S(1)}, f32[288]{0:T(512)}, u32[]{:S(2)}) copy-start(f32[288]{0:T(512)} %get-tuple-element.1316) | copy-start | bytes 3460 | tf_op jit(solution)/shard_map/while
  1146.7 19.5 %copy-start.31 = (f32[288]{0:T(512)S(1)}, f32[288]{0:T(512)}, u32[]{:S(2)}) copy-start(f32[288]{0:T(512)} %get-tuple-element.1315) | copy-start | bytes 3460 | tf_op jit(solution)/shard_map/while
  1155.4 13.4 copy-start.17
  1155.4 13.4 copy-start.19
  1155.4 13.4 copy-start.38
  1155.4 13.4 copy-start.40
  1172.0 133.5 %all-reduce.13.cloned.1.call-start = ((), (), s32[]{:S(2)}) async-start(), calls=%async_computation.5 | async-start | bytes 11280384 | tf_op jit(solution)/shard_map/psum | solution.py:299
  1180.3 270.4 %all-gather.5.cloned.1.call-start = ((), (), s32[]{:S(2)}) async-start(), calls=%async_computation.4 | async-start | bytes 17915904 | tf_op jit(solution)/shard_map/all_gather | solution.py:292
  (129 other events, 673.6 us)
Sparse Core Ops, SparseCore 0:
  64.7 35.1 reduce-scatter.4
  111.7 32.4 all-gather.6
  161.8 32.4 reduce-scatter.8
  208.8 32.4 all-gather.8
  244.1 32.4 reduce-scatter.6
  279.5 32.4 reduce-scatter.10
  348.5 32.4 reduce-scatter.4
  392.8 32.4 all-gather.6
  442.9 32.4 reduce-scatter.8
  489.8 32.4 all-gather.8
  525.3 32.4 reduce-scatter.6
  560.8 32.4 reduce-scatter.10
  629.5 32.4 reduce-scatter.4
  673.8 32.4 all-gather.6
  723.9 32.4 reduce-scatter.8
  770.8 32.4 all-gather.8
  806.2 32.4 reduce-scatter.6
  841.6 32.4 reduce-scatter.10
  910.6 32.4 reduce-scatter.4
  954.9 32.4 all-gather.6
  1005.0 32.4 reduce-scatter.8
  1051.9 32.4 all-gather.8
  1087.4 32.4 reduce-scatter.6
  1122.8 32.4 reduce-scatter.10
Sparse Core Ops, SparseCore 1:
  1180.4 125.0 all-reduce.12
  1307.0 143.7 all-gather.4
